TPU v7x, 32 devices: a whole 2x2x4 slice. The times are simulated.
32 devices in a mesh: rep: 1, dp: 32 (over x, y, z, core).
Axes of the slice: x: 2, y: 2, z: 4, core: 2. Of those that a mesh axis runs over, the one named last changes fastest.
Arguments:
- x: bfloat16 [32, 2048, 1280], P(('rep', 'dp'))
- dy: bfloat16 [32, 2048, 1280], P(('rep', 'dp'))
- w_gate: bfloat16 [2, 1280, 3072], replicated
- w_up: bfloat16 [2, 1280, 3072], replicated
- w_down: bfloat16 [2, 3072, 1280], replicated
- m_w_gate: float32 [2, 1280, 3072], P(None, 'dp')
- m_w_up: float32 [2, 1280, 3072], P(None, 'dp')
- m_w_down: float32 [2, 3072, 1280], P(None, 'dp')
- v_w_gate: float32 [2, 1280, 3072], P(None, 'dp')
- v_w_up: float32 [2, 1280, 3072], P(None, 'dp')
- v_w_down: float32 [2, 3072, 1280], P(None, 'dp')
Outputs:
- output 1: bfloat16 [2, 1280, 3072], P('rep')
- output 2: bfloat16 [2, 1280, 3072], P('rep')
- output 3: bfloat16 [2, 3072, 1280], P('rep')
- output 4: float32 [2, 1280, 3072], P('rep', 'dp')
- output 5: float32 [2, 1280, 3072], P('rep', 'dp')
- output 6: float32 [2, 3072, 1280], P('rep', 'dp')
- output 7: float32 [2, 1280, 3072], P('rep', 'dp')
- output 8: float32 [2, 1280, 3072], P('rep', 'dp')
- output 9: float32 [2, 3072, 1280], P('rep', 'dp')
All inputs are finite; a program needn't handle non-finite values.
Results may differ from a plain program's by a relative error of at most 0.022.
Values are sent between devices in bfloat16 or wider.
A program may use at most 2 GiB of HBM per device.

v0:
```python
import jax
import jax.numpy as jnp
from jax import lax

NAMES = ("w_gate", "w_up", "w_down")


def matmul(a, w):
    return jnp.dot(a, w, preferred_element_type=jnp.float32).astype(jnp.bfloat16)


def normed(h):
    wide = h.astype(jnp.float32)
    scale = lax.rsqrt(jnp.mean(wide**2, -1, keepdims=True) + 1e-6)
    return (wide * scale).astype(jnp.bfloat16)


def layer(h, w):
    a = normed(h)
    gate = jnp.dot(a, w["w_gate"], preferred_element_type=jnp.float32)
    up = jnp.dot(a, w["w_up"], preferred_element_type=jnp.float32)
    return h + matmul((jax.nn.silu(gate) * up).astype(jnp.bfloat16), w["w_down"])


def adamw(w, m, v, g):
    m = 0.9 * m + 0.1 * g
    v = 0.95 * v + 0.05 * g * g
    step = m * lax.rsqrt(v + 1e-8) + 0.1 * w
    return (w - 0.02 * step).astype(jnp.bfloat16), m, v


def clipped(gradients, sum_of_squares, count):
    factor = jnp.minimum(1.0, 0.5 * lax.rsqrt(sum_of_squares / count + 1e-30))
    return [g * factor for g in gradients]


def stack(weights, h):
    for number in range(weights["w_gate"].shape[0]):
        h = layer(h, {name: w[number] for name, w in weights.items()})
    return h


def solution(mesh):
    groups = mesh.shape["rep"]

    def step(x, dy, *arrays):
        weights, m, v = (arrays[i : i + 3] for i in (0, 3, 6))
        x, dy = (t.reshape(groups, -1, *t.shape[1:]) for t in (x, dy))

        def of_a_group(x, dy):
            _, back = jax.vjp(lambda w: stack(w, x), dict(zip(NAMES, weights, strict=True)))
            by_weights = back(dy)[0]
            gradients = [by_weights[name].astype(jnp.float32) for name in NAMES]
            gradients = clipped(gradients, sum(jnp.sum(g * g) for g in gradients), sum(g.size for g in gradients))
            new = [adamw(w.astype(jnp.float32), m, v, g) for w, m, v, g in zip(weights, m, v, gradients, strict=True)]
            return tuple(one[which] for which in range(3) for one in new)

        return tuple(t.reshape(-1, *t.shape[2:]) for t in jax.vmap(of_a_group)(x, dy))

    return step
```

profile of v0, /device:TPU:0, one launch (start us, length us, event | category | flops | bytes accessed | tf_op | source)
XLA Modules:
  0.0 2513.8 jit_solution(17631993697941457193)
XLA Ops:
  7.2 7.9 copy.1
  25.8 20.4 fusion.173
  46.1 34.8 %fusion.150 = (bf16[1,2048,3072]{2,1,0:T(8,128)(2,1)}, f32[2048,3072]{1,0:T(8,128)}) fusion(f32[2048,3072]{1,0:T(8,128)} %fusion.173, bf16[2,1280,3072]{2,1,0:T(8,128)(2,1)} %param.17, bf16[1,2048,1280]{1,2,0:T(8,128)(2,1)} %copy-done), kind=kOutput, calls=%fused_computation.189 | convolution fusion | flops 16143876096 | bytes 76021760 | tf_op jit(solution)/vmap(jvp())/dot_general | solution.py:21
  81.0 22.7 fusion.160
  108.4 22.0 fusion.166
  130.4 22.0 convolution_convert_fusion.1
  152.4 43.5 %fusion.139 = (bf16[1,2048,3072]{2,1,0:T(8,128)(2,1)}, bf16[1,2048,3072]{2,1,0:T(8,128)(2,1)}, f32[2048,3072]{1,0:T(8,128)}) fusion(f32[2048,3072]{1,0:T(8,128)} %fusion.166, bf16[2048,3072]{1,0:T(8,128)(2,1)} %convolution_convert_fusion.1, bf16[2,1280,3072]{2,1,0:T(8,128)(2,1)} %param.12, bf16[1,2048,1280]{1,2,0:T(8,128)(2,1)} %copy-done.1), kind=kOutput, calls=%fused_computation.173 | convolution fusion | flops 16200499200 | bytes 101187584 | tf_op jit(solution)/vmap(jvp())/dot_general | solution.py:20
  195.9 21.6 fusion.149
  217.5 16.7 copy.3
  234.2 283.3 %while.16 = (bf16[1,2048,3072]{1,2,0:T(8,128)(2,1)}, bf16[1,2048,1280]{2,1,0:T(8,128)(2,1)}, f32[96,1280]{1,0:T(8,128)S(1)}, f32[96,1280]{1,0:T(8,128)}, u32[]{:...) while((bf16[1,2048,3072]{1,2,0:T(8,128)(2,1)}, ...), condition=%wide.windowed_dot_general_cond_rs.4.clone, body=%wide.windowed_dot_general_body_rs.4.clone.sunk | while | flops 2017148928 | bytes 53346896 | solution.py:9
  518.3 8.3 copy.2
  526.7 16.7 copy.5
  543.4 21.5 fusion.184
  564.9 23.7 fusion.162
  588.7 12.3 fusion.220
  601.0 7.9 copy.4
  608.9 284.9 %while.17 = (bf16[1,2048,1280]{2,1,0:T(8,128)(2,1)}, bf16[1,2048,3072]{1,2,0:T(8,128)(2,1)}, f32[1280,96]{0,1:T(8,128)S(1)}, f32[1280,96]{0,1:T(8,128)}, u32[]{:...) while((bf16[1,2048,1280]{2,1,0:T(8,128)(2,1)}, ...), condition=%wide.windowed_dot_general_cond_rs.5.clone, body=%wide.windowed_dot_general_body_rs.5.clone.sunk | while | flops 2017148928 | bytes 53346896 | solution.py:9
  669.7 7.8 collective-permute-done.22
  741.5 7.8 collective-permute-done.22
  813.3 7.8 collective-permute-done.22
  894.6 276.2 %while.14 = (bf16[1,2048,3072]{2,1,0:T(8,128)(2,1)}, bf16[1,2048,1280]{1,2,0:T(8,128)(2,1)}, f32[3072,40]{0,1:T(8,128)S(1)}, f32[3072,40]{0,1:T(8,128)}, u32[]{:...) while((bf16[1,2048,3072]{2,1,0:T(8,128)(2,1)}, ...), condition=%wide.windowed_dot_general_cond_rs.2.clone, body=%wide.windowed_dot_general_body_rs.2.clone.sunk | while | flops 2015313920 | bytes 53346896 | solution.py:21
  907.3 9.0 collective-permute-done.8
  1171.6 39.8 %convert_multiply_fusion = (bf16[1,2048,3072]{2,1,0:T(8,128)(2,1)}, bf16[1,2048,3072]{2,1,0:T(8,128)(2,1)}) fusion(f32[2048,3072]{1,0:T(8,128)} %fusion.173, f32[2048,3072]{1,0:T(8,128)} %get-tuple-element.264, bf16[2,3072,1280]{2,1,0:T(8,128)(2,1)} %param.15, bf16[1,2048,1280]{1,2,0:T(8,128)(2,1)} %fusion.220), kind=kOutput, calls=%fused_computation.168 | convolution fusion | flops 16206790656 | bytes 88604672 | tf_op jit(solution)/vmap(transpose(jvp()))/dot_general | solution.py:9
  1211.4 279.8 %while.15 = (bf16[1,2048,3072]{2,1,0:T(8,128)(2,1)}, bf16[1,2048,1280]{1,2,0:T(8,128)(2,1)}, f32[3072,40]{0,1:T(8,128)S(1)}, f32[3072,40]{0,1:T(8,128)S(1)}, u32...) while((bf16[1,2048,3072]{2,1,0:T(8,128)(2,1)}, ...), condition=%wide.windowed_dot_general_cond_rs.3.clone, body=%wide.windowed_dot_general_body_rs.3.clone.sunk | while | flops 2015313920 | bytes 55313004 | solution.py:21
  1491.9 276.4 %while.12 = (bf16[1,2048,3072]{2,1,0:T(8,128)(2,1)}, bf16[1,2048,1280]{1,2,0:T(8,128)(2,1)}, f32[3072,40]{0,1:T(8,128)S(1)}, f32[3072,40]{0,1:T(8,128)S(1)}, u32...) while((bf16[1,2048,3072]{2,1,0:T(8,128)(2,1)}, ...), condition=%wide.windowed_dot_general_cond_rs.clone, body=%wide.windowed_dot_general_body_rs.clone.sunk | while | flops 2015313920 | bytes 53346896 | solution.py:20
  1769.2 303.0 %while.13 = (bf16[1,2048,3072]{2,1,0:T(8,128)(2,1)}, bf16[1,2048,1280]{1,2,0:T(8,128)(2,1)}, f32[3072,40]{0,1:T(8,128)S(1)}, f32[3072,40]{0,1:T(8,128)}, u32[]{:...) while((bf16[1,2048,3072]{2,1,0:T(8,128)(2,1)}, ...), condition=%wide.windowed_dot_general_cond_rs.1.clone, body=%wide.windowed_dot_general_body_rs.1.clone.sunk | while | flops 2015313920 | bytes 55313004 | solution.py:20
  2097.4 38.1 %all-reduce.10 = f32[]{:T(128)} all-reduce(f32[]{:T(128)S(6)} %add.180), channel_id=13, replica_groups=mesh['rep'=1,'dp'=32] {'dp'}, use_global_device_ids=true, to_apply=%region_3.4.clone | all-reduce | flops 1 | bytes 8 | tf_op jit(solution)/vmap()/reduce_sum | solution.py:54
  2146.9 104.7 %all-gather.14.cloned.1.call-done = bf16[1,2,3072,1280]{3,2,1,0:T(8,128)(2,1)} async-done(((bf16[1,2,96,1280]{3,2,1,0:T(8,128)(2,1)}), bf16[1,2,3072,1280]{3,2,1,0:T(8,128)(2,1)}) %all-gather.14.cloned.1.call-update) | async-done | bytes 15728656 | tf_op jit(solution)/reshape | solution.py:58
  2251.6 111.6 %all-gather.12.cloned.1.call-done = bf16[1,2,1280,3072]{3,2,1,0:T(8,128)(2,1)} async-done(((bf16[1,2,40,3072]{3,2,1,0:T(8,128)(2,1)}), bf16[1,2,1280,3072]{3,2,1,0:T(8,128)(2,1)}) %all-gather.12.cloned.1.call-update) | async-done | bytes 15728656 | tf_op jit(solution)/reshape | solution.py:58
  2363.2 111.6 %all-gather.10.cloned.1.call-done = bf16[1,2,1280,3072]{3,2,1,0:T(8,128)(2,1)} async-done(((bf16[1,2,40,3072]{3,2,1,0:T(8,128)(2,1)}), bf16[1,2,1280,3072]{3,2,1,0:T(8,128)(2,1)}) %all-gather.10.cloned.1.call-update) | async-done | bytes 15728656 | tf_op jit(solution)/reshape | solution.py:58
  2474.8 15.9 copy.63
  2490.6 8.0 copy.64
  (807 shorter events, 1730.2 us)
Async XLA Ops:
  7.2 2244.4 %all-gather.14.cloned.1.call-start = ((), (), s32[]{:S(2)}) async-start(), calls=%async_computation.2 | async-start | bytes 16220160 | tf_op jit(solution)/reshape | solution.py:58
  517.5 1554.6 %collective-permute-start.28 = (f32[96,1280]{1,0:T(8,128)}, f32[96,1280]{1,0:T(8,128)}, u32[]{:S(2)}, u32[]{:S(2)}) collective-permute-start(f32[96,1280]{1,0:T(8,128)} %get-tuple-element.45), channel_id=32, source_target_pairs={{0,1},{1,2},{2,3},{3,4},{4,5},{5,6},{6,7},{7,8},{8,9},{9,10},{10,1... | collective-permute-start | bytes 1474568 | tf_op jit(solution)/vmap(transpose(jvp()))/dot_general | solution.py:9
  660.3 17.1 collective-permute-start.22
  732.1 17.1 collective-permute-start.22
  804.0 17.1 collective-permute-start.22
  875.8 17.1 collective-permute-start.22
  893.8 1179.5 %collective-permute-start.29 = (f32[1280,96]{0,1:T(8,128)}, f32[1280,96]{0,1:T(8,128)}, u32[]{:S(2)}, u32[]{:S(2)}) collective-permute-start(f32[1280,96]{0,1:T(8,128)} %get-tuple-element.47), channel_id=38, source_target_pairs={{0,1},{1,2},{2,3},{3,4},{4,5},{5,6},{6,7},{7,8},{8,9},{9,10},{10,1... | collective-permute-start | bytes 1474568 | tf_op jit(solution)/vmap(transpose(jvp()))/dot_general | solution.py:9
  894.7 21.6 collective-permute-start.8
  894.8 21.5 collective-permute-start.9
  948.4 17.1 collective-permute-start.10
  948.5 17.1 collective-permute-start.11
  1170.8 904.5 %collective-permute-start.26 = (f32[3072,40]{0,1:T(8,128)}, f32[3072,40]{0,1:T(8,128)}, u32[]{:S(2)}, u32[]{:S(2)}) collective-permute-start(f32[3072,40]{0,1:T(8,128)} %get-tuple-element.41), channel_id=19, source_target_pairs={{0,1},{1,2},{2,3},{3,4},{4,5},{5,6},{6,7},{7,8},{8,9},{9,10},{10,1... | collective-permute-start | bytes 1474568 | tf_op jit(solution)/vmap(transpose(jvp()))/dot_general | solution.py:21
  1299.5 17.4 collective-permute-start.15
  1334.1 17.4 collective-permute-start.15
  1368.7 17.4 collective-permute-start.15
  1403.3 17.4 collective-permute-start.15
  1437.9 17.4 collective-permute-start.15
  1472.5 17.4 collective-permute-start.15
  1595.0 17.1 collective-permute-start
  1664.4 17.1 collective-permute-start
  1733.7 17.1 collective-permute-start
  1825.5 17.5 collective-permute-start.7
  1863.4 17.2 collective-permute-start.7
  1901.2 17.5 collective-permute-start.7
  1939.0 17.2 collective-permute-start.7
  1976.9 17.5 collective-permute-start.7
  2014.7 17.2 collective-permute-start.7
  2052.5 17.5 collective-permute-start.7
  2072.1 17.1 collective-permute-start.24
  2072.2 22.4 collective-permute-start.25
  2139.8 223.4 %all-gather.12.cloned.1.call-start = ((), (), s32[]{:S(2)}) async-start(), calls=%async_computation.1 | async-start | bytes 16220160 | tf_op jit(solution)/reshape | solution.py:58
  2143.5 331.3 %all-gather.10.cloned.1.call-start = ((), (), s32[]{:S(2)}) async-start(), calls=%async_computation | async-start | bytes 16220160 | tf_op jit(solution)/reshape | solution.py:58
  (212 other events, 3935.5 us)
Sparse Core Ops, SparseCore 0:
  2139.9 111.6 all-gather.13
  2255.2 107.9 all-gather.11
  2366.8 107.9 all-gather.9
where the time goes:
time: 2530 us; the launch traced here: 2510 us
  matrix products  828 us (33%)
  waiting for transfers between devices  783 us (31%)
  starting transfers between devices  521 us (21%)
  other arithmetic  214 us (8%)
  local copies, waits for them, and re-layouts  111 us (4%)
  blocking collectives  38.1 us (2%)
    reshape x3, waiting for transfers between devices, step(): t.reshape(-1, *t.shape[2:])  328 us
    dot_general x35, matrix products, layer(): gate = jnp.dot(a, w['w_gate'], preferred_element_type=jnp.float32)  313 us
    dot_general x35, matrix products, layer(): up = jnp.dot(a, w['w_up'], preferred_element_type=jnp.float32)  304 us
    dot_general x66, waiting for transfers between devices, matmul(): jnp.dot(a, w, preferred_element_type=jnp.float32).astype(jnp.bfloat16)  235 us
    dot_general x35, matrix products, matmul(): jnp.dot(a, w, preferred_element_type=jnp.float32).astype(jnp.bfloat16)  210 us
    dot_general x66, starting transfers between devices, matmul(): jnp.dot(a, w, preferred_element_type=jnp.float32).astype(jnp.bfloat16)  175 us
    dot_general x66, starting transfers between devices, layer(): up = jnp.dot(a, w['w_up'], preferred_element_type=jnp.float32)  174 us
    dot_general x66, starting transfers between devices, layer(): gate = jnp.dot(a, w['w_gate'], preferred_element_type=jnp.float32)  172 us
  transfers between devices with their start and end apart: 201, of which 104 were waited for; matrix products, arithmetic and copies ran while one was open for 34% of the time, Pallas kernels for 0%

commit v1 on v0

--- a/solution.py
+++ b/solution.py
@@ -1,6 +1,12 @@
+import functools
+
 import jax
 import jax.numpy as jnp
 from jax import lax
+from jax.experimental import pallas as pl
+from jax.experimental.pallas import tpu as pltpu
+from jax.sharding import PartitionSpec as P
+
 
 NAMES = ("w_gate", "w_up", "w_down")
 
@@ -40,21 +46,106 @@
     return h
 
 
+MESHID = pl.DeviceIdType.MESH
+def place():
+    me = lax.axis_index("dp")
+    return (me // 16) % 2, (me // 8) % 2, (me // 4) % 2, (me // 2) % 2, me % 2
+MASK = (16, 8, 4, 2, 1)
+def partner(pos, dim):
+    me = lax.axis_index("dp")
+    return me + MASK[dim] * (1 - 2 * pos[dim])
+def dev(i): return {"rep": 0, "dp": i}
+X, Y, ZH, ZL, C = range(5)
+GATHER = ((ZH, ZL, Y, X, C), (ZH, X, ZL, Y, C), (ZH, Y, X, ZL, C))
+
+def barrier(pos, dims):
+    bar = pltpu.get_barrier_semaphore()
+    for d in dims:
+        pl.semaphore_signal(bar, inc=1, device_id=dev(partner(pos, d)), device_id_type=MESHID)
+    pl.semaphore_wait(bar, len(dims))
+
+def streams(sizes):
+    groups = []
+    for layer in (0, 1):
+        for i in (0, 1, 2):
+            for lo, parts in sizes[i]:
+                g = []
+                for colour, n in enumerate(parts):
+                    g.append((i, layer, lo, n, colour)); lo += n
+                groups.append(g)
+    return groups
+
+def gather_kernel(groups, own, out, send, recv, local):
+    pos = place()
+    for i in range(3):
+        pass
+    barrier(pos, range(5))
+    me = tuple(pos)
+    first = []
+    for i in range(3):
+        cp = pltpu.make_async_copy(own[i], out[i].at[(slice(None), *me)], local.at[i]); cp.start(); first.append(cp)
+    def copy(n, s, phase):
+        i, layer, lo, cols, colour = s
+        order = GATHER[colour]
+        done = order[:phase]
+        d = order[phase]
+        cs = pl.ds(lo, cols)
+        if phase == 0:
+            src = own[i].at[layer, :, cs]
+        index = (layer, *(slice(None) if k in done else pos[k] for k in range(5)), slice(None), cs)
+        dst = out[i].at[index]
+        if phase: src = dst
+        return pltpu.make_async_remote_copy(src_ref=src, dst_ref=dst, send_sem=send.at[n, phase], recv_sem=recv.at[n, phase],
+                                            device_id=dev(partner(pos, d)), device_id_type=MESHID)
+    started = []
+    for k in range(len(groups) + 5):
+        for g in range(len(groups)):
+            phase = k - g
+            if 0 <= phase <= 5:
+                for j, s in enumerate(groups[g]):
+                    n = 3 * g + j
+                    if phase > 0: copy(n, s, phase - 1).wait_recv()
+                    if phase == 1 and g == 0 and j == 0:
+                        for cp in first: cp.wait()
+                    if phase < 5:
+                        c = copy(n, s, phase); c.start(); started.append(c)
+    for c in started: c.wait_send()
+
+SIZES = (((0, (1280, 1152, 640)),), ((0, (1280, 1152, 640)),), ((0, (512, 512, 256)),))
+SIZES2 = (((0, (640, 640, 256)), (1536, (640, 512, 384))), ((0, (640, 640, 256)), (1536, (640, 512, 384))), ((0, (256, 256, 128)), (640, (256, 256, 128))))
+def gather(own, sizes=SIZES):
+    groups = streams(sizes)
+    n = 3 * len(groups)
+    def kernel(*refs):
+        gather_kernel(groups, refs[:3], refs[3:6], *refs[6:])
+    out = pl.pallas_call(kernel,
+        out_shape=[jax.ShapeDtypeStruct((2, 2, 2, 2, 2, 2, *o.shape[1:]), o.dtype) for o in own],
+        in_specs=[pl.BlockSpec(memory_space=pltpu.VMEM)] * 3, out_specs=[pl.BlockSpec(memory_space=pl.ANY)] * 3,
+        scratch_shapes=[pltpu.SemaphoreType.DMA((n, 5)), pltpu.SemaphoreType.DMA((n, 5)), pltpu.SemaphoreType.DMA((3,))],
+        compiler_params=pltpu.CompilerParams(collective_id=3, has_side_effects=True))(*own)
+    return [o.reshape(2, -1, o.shape[-1]) for o in out]
+
+
 def solution(mesh):
-    groups = mesh.shape["rep"]
-
     def step(x, dy, *arrays):
         weights, m, v = (arrays[i : i + 3] for i in (0, 3, 6))
-        x, dy = (t.reshape(groups, -1, *t.shape[1:]) for t in (x, dy))
+        x, dy = x[0], dy[0]
+        _, back = jax.vjp(lambda w: stack(w, x), dict(zip(NAMES, weights, strict=True)))
+        by_weights = back(dy)[0]
+        gradients = [lax.psum_scatter(by_weights[name], "dp", scatter_dimension=1, tiled=True).astype(jnp.float32) for name in NAMES]
+        squares = lax.psum(sum(jnp.sum(g * g) for g in gradients), "dp")
+        gradients = clipped(gradients, squares, sum(w.size for w in weights))
+        me = lax.axis_index("dp")
+        own = [lax.dynamic_slice_in_dim(w, me * g.shape[1], g.shape[1], 1) for w, g in zip(weights, gradients)]
+        new = [adamw(w.astype(jnp.float32), m, v, g) for w, m, v, g in zip(own, m, v, gradients, strict=True)]
+        full = gather([one[0] for one in new])
+        return (*full, *(one[1] for one in new), *(one[2] for one in new))
 
-        def of_a_group(x, dy):
-            _, back = jax.vjp(lambda w: stack(w, x), dict(zip(NAMES, weights, strict=True)))
-            by_weights = back(dy)[0]
-            gradients = [by_weights[name].astype(jnp.float32) for name in NAMES]
-            gradients = clipped(gradients, sum(jnp.sum(g * g) for g in gradients), sum(g.size for g in gradients))
-            new = [adamw(w.astype(jnp.float32), m, v, g) for w, m, v, g in zip(weights, m, v, gradients, strict=True)]
-            return tuple(one[which] for which in range(3) for one in new)
-
-        return tuple(t.reshape(-1, *t.shape[2:]) for t in jax.vmap(of_a_group)(x, dy))
-
-    return step
+    data, whole, shard = P(("rep", "dp")), P(), P(None, "dp")
+    return jax.shard_map(
+        step,
+        mesh=mesh,
+        in_specs=(data, data, *[whole] * 3, *[shard] * 6),
+        out_specs=(*[P("rep")] * 3, *[P("rep", "dp")] * 6),
+        check_vma=False,
+    )

time: 2530 us -> 1240 us (0.49)
  starting transfers between devices: 521 us -> 0.12 us
  waiting for transfers between devices: 783 us -> 307 us
  matrix products: 828 us -> 389 us
  Pallas kernels: 0 us -> 194 us
  other arithmetic: 214 us -> 55.9 us
  local copies, waits for them, and re-layouts: 111 us -> 228 us
    dot_general x198 -> x0, starting transfers between devices: 521 us -> none  [the longest x66 175 us: matmul(): jnp.dot(a, w, preferred_element_type=jnp.float32).astype(jnp.bfloat16)]
    dot_general x198 -> x0, waiting for transfers between devices: 455 us -> none  [the longest x66 235 us: matmul(): jnp.dot(a, w, preferred_element_type=jnp.float32).astype(jnp.bfloat16)]
    reshape x3 -> x0, waiting for transfers between devices: 328 us -> none  [step(): t.reshape(-1, *t.shape[2:])]
    pallas_call x0 -> x1, Pallas kernels: none -> 194 us  [gather(): pl.pallas_call(kernel, out_shape=[jax.ShapeDtypeStruct((2, 2, 2, 2, 2, 2,...]
    dot_general x35 -> x5, matrix products: 313 us -> 137 us  [layer(): gate = jnp.dot(a, w['w_gate'], preferred_element_type=jnp.float32)]
    reduce_scatter x0 -> x1, waiting for transfers between devices: none -> 172 us  [step(): lax.psum_scatter(by_weights[name], 'dp', scatter_dimension=1, tiled=True)]
    dot_general x35 -> x5, matrix products: 304 us -> 133 us  [layer(): up = jnp.dot(a, w['w_up'], preferred_element_type=jnp.float32)]
    dot_general x192 -> x0, other arithmetic: 152 us -> none  [the longest x32 57.3 us: layer(): gate = jnp.dot(a, w['w_gate'], preferred_element_type=jnp.float32)]
  transfers between devices with their start and end apart: 201 -> 3, of which waited for: 104 -> 2; matrix products, arithmetic and copies ran while one was open for 34% -> 18% of each run, Pallas kernels for 0% -> 0%
where the time goes in v1:
time: 1240 us; the launch traced here: 1230 us
  matrix products  389 us (31%)
  waiting for transfers between devices  307 us (25%)
  local copies, waits for them, and re-layouts  228 us (18%)
  Pallas kernels  194 us (16%)
  other arithmetic  55.9 us (5%)
  blocking collectives  40.9 us (3%)
  between operations  17.1 us (1%)
    unnamed x45, local copies, waits for them, and re-layouts  228 us
    pallas_call x1, Pallas kernels, gather(): pl.pallas_call(kernel, out_shape=[jax.ShapeDtypeStruct((2, 2, 2, 2, 2, 2,...  194 us
    reduce_scatter x1, waiting for transfers between devices, step(): lax.psum_scatter(by_weights[name], 'dp', scatter_dimension=1, tiled=True)  172 us
    dot_general x5, matrix products, layer(): gate = jnp.dot(a, w['w_gate'], preferred_element_type=jnp.float32)  137 us
    unnamed x5, waiting for transfers between devices  135 us
    dot_general x5, matrix products, layer(): up = jnp.dot(a, w['w_up'], preferred_element_type=jnp.float32)  133 us
    dot_general x5, matrix products, matmul(): jnp.dot(a, w, preferred_element_type=jnp.float32).astype(jnp.bfloat16)  119 us
    psum x1, blocking collectives, step(): squares = lax.psum(sum((jnp.sum(g * g) for g in gradients)), 'dp')  40.9 us
  transfers between devices with their start and end apart: 3, of which 2 were waited for; matrix products, arithmetic and copies ran while one was open for 18% of the time, Pallas kernels for 0%

profile of v1, /device:TPU:0, one launch (start us, length us, event | category | flops | bytes accessed | tf_op | source)
XLA Modules:
  0.0 1232.5 jit_solution(1862542537924545135)
XLA Ops:
  7.2 7.9 copy.22
  18.7 8.0 copy.23
  26.7 22.4 %convolution_convert_fusion.2 = bf16[2048,3072]{1,0:T(8,128)(2,1)} fusion(bf16[2,3072,1280]{2,1,0:T(8,128)(2,1)} %param.15, bf16[1,2048,1280]{2,1,0:T(8,128)(2,1)} %param.12), kind=kOutput, calls=%fused_computation.39 | convolution fusion | flops 16112418816 | bytes 25690112 | tf_op jit(solution)/shard_map/transpose(jvp())/dot_general | solution.py:15
  49.2 21.6 %fusion.49 = f32[2048,3072]{1,0:T(8,128)} fusion(bf16[2,1280,3072]{2,1,0:T(8,128)(2,1)} %param.13, bf16[1,2048,1280]{2,1,0:T(8,128)(2,1)S(1)} %bitcast.103, f32[2048]{0:T(1024)S(1)} %add_rsqrt_fusion), kind=kOutput, calls=%fused_computation.69 | convolution fusion | flops 16113991680 | bytes 38281216 | tf_op jit(solution)/shard_map/jvp()/dot_general | solution.py:26
  70.8 35.0 %multiply_convert_fusion.1 = (bf16[2048,3072]{1,0:T(8,128)(2,1)}, f32[2048,3072]{1,0:T(8,128)}) fusion(f32[2048,3072]{1,0:T(8,128)} %fusion.49, bf16[2,1280,3072]{2,1,0:T(8,128)(2,1)} %param.14, bf16[1,2048,1280]{2,1,0:T(8,128)(2,1)} %param.11, f32[2048]{0:T(1024)S(1)} %add_rsqrt_fusion), kind=kOutput, calls=%fused_computation.17 | convolution fusion | flops 16151740416 | bytes 76029952 | tf_op jit(solution)/shard_map/jvp()/dot_general | solution.py:27
  105.8 22.5 %fusion.25 = (f32[2048]{0:T(1024)S(1)}, bf16[2048,1280]{0,1:T(8,128)(2,1)S(1)}) fusion(bf16[2048,3072]{1,0:T(8,128)(2,1)} %get-tuple-element.24, bf16[2,3072,1280]{2,1,0:T(8,128)(2,1)} %param.15, bf16[1,2048,1280]{1,2,0:T(8,128)(2,1)} %copy.22), kind=kOutput, calls=%fused_computation.46 | convolution fusion | flops 16119232512 | bytes 30941184 | tf_op jit(solution)/shard_map/jvp()/dot_general | solution.py:15
  130.6 22.1 %fusion.41 = f32[2048,3072]{1,0:T(8,128)} fusion(bf16[2,1280,3072]{2,1,0:T(8,128)(2,1)} %param.14, bf16[2048,1280]{0,1:T(8,128)(2,1)S(1)} %get-tuple-element.27, f32[2048]{0:T(1024)S(1)} %fusion.109), kind=kOutput, calls=%fused_computation.61 | convolution fusion | flops 16113991680 | bytes 38281216 | tf_op jit(solution)/shard_map/jvp()/dot_general | solution.py:27
  152.7 38.5 %fusion.2 = (bf16[2048,3072]{1,0:T(8,128)(2,1)}, f32[2048,3072]{1,0:T(8,128)}) fusion(f32[2048,3072]{1,0:T(8,128)} %fusion.41, bf16[2048,3072]{1,0:T(8,128)(2,1)} %convolution_convert_fusion.2, bf16[2,1280,3072]{2,1,0:T(8,128)(2,1)} %param.13, bf16[2048,1280]{0,1:T(8,128)(2,1)} %copy-done.1, f32[2048]{0:T(1024)S(1)} %fusion.109), kind=kOutput, calls=%fused_computation.8 | convolution fusion | flops 16189489152 | bytes 88612864 | tf_op jit(solution)/shard_map/jvp()/dot_general | solution.py:26
  191.2 22.7 %fusion.57 = bf16[2048,1280]{0,1:T(8,128)(2,1)} fusion(bf16[2048,3072]{1,0:T(8,128)(2,1)} %get-tuple-element.28, bf16[2,1280,3072]{2,1,0:T(8,128)(2,1)} %param.13), kind=kOutput, calls=%fused_computation.75 | convolution fusion | flops 16106127360 | bytes 25690112 | tf_op jit(solution)/shard_map/transpose(jvp())/dot_general | solution.py:26
  213.9 23.7 %fusion.33 = bf16[1,1280,3072]{2,1,0:T(8,128)(2,1)} fusion(bf16[2048,3072]{1,0:T(8,128)(2,1)} %convolution_convert_fusion.2, bf16[2048,1280]{0,1:T(8,128)(2,1)S(1)} %copy-done.2, f32[2048]{0:T(1024)S(1)} %fusion.109, f32[2048,3072]{1,0:T(8,128)} %get-tuple-element.29), kind=kOutput, calls=%fused_computation.53 | convolution fusion | flops 16155672576 | bytes 50864128 | tf_op jit(solution)/shard_map/transpose(jvp())/dot_general | solution.py:27
  237.6 28.5 %fusion.27 = (f32[2048]{0:T(1024)S(1)}, bf16[2048,1280]{0,1:T(8,128)(2,1)}) fusion(bf16[2048,1280]{0,1:T(8,128)(2,1)} %copy-done.1, bf16[2048,1280]{0,1:T(8,128)(2,1)} %fusion.57, bf16[2,1280,3072]{2,1,0:T(8,128)(2,1)} %param.14, bf16[2048,3072]{1,0:T(8,128)(2,1)} %convolution_convert_fusion.2, f32[2048,3072]{1,0:T(8,128)} %get-tuple-element.29), kind=kOutput, calls=%fused_computation.48 | convolution fusion | flops 16159602688 | bytes 61349888 | tf_op jit(solution)/shard_map/transpose(jvp())/dot_general | solution.py:27
  266.1 12.5 %fusion.76 = bf16[2048,1280]{0,1:T(8,128)(2,1)} fusion(bf16[2048,1280]{0,1:T(8,128)(2,1)} %copy-done.1, bf16[2048,1280]{0,1:T(8,128)(2,1)} %get-tuple-element.31, bf16[1,2048,1280]{1,2,0:T(8,128)(2,1)} %copy.23, f32[2048]{0:T(1024)S(1)} %multiply_multiply_fusion.3, f32[2048]{0:T(1024)S(1)} %fusion.109), kind=kLoop, calls=%fused_computation.86 | loop fusion | flops 18350080 | bytes 20987904 | tf_op jit(solution)/shard_map/transpose(jvp())/add_any | solution.py:19
  278.6 23.0 %convolution_convert_fusion.1 = bf16[2048,3072]{1,0:T(8,128)(2,1)} fusion(bf16[2048,1280]{0,1:T(8,128)(2,1)} %fusion.76, bf16[2,3072,1280]{2,1,0:T(8,128)(2,1)} %param.15), kind=kOutput, calls=%fused_computation.38 | convolution fusion | flops 16112418816 | bytes 25690112 | tf_op jit(solution)/shard_map/transpose(jvp())/dot_general | solution.py:15
  301.6 23.7 %fusion.32 = bf16[1,1280,3072]{2,1,0:T(8,128)(2,1)} fusion(bf16[2048,3072]{1,0:T(8,128)(2,1)} %convolution_convert_fusion.1, bf16[1,2048,1280]{1,2,0:T(8,128)(2,1)S(1)} %bitcast.96, f32[2048]{0:T(1024)S(1)} %copy-done.8, f32[2048,3072]{1,0:T(8,128)} %fusion.49), kind=kOutput, calls=%fused_computation.52 | convolution fusion | flops 16155672576 | bytes 50864128 | tf_op jit(solution)/shard_map/transpose(jvp())/dot_general | solution.py:27
  325.4 7.5 pad_add_fusion.1
  332.9 72.0 %copy.26 = bf16[2,1280,3072]{2,0,1:T(2,128)(2,1)} copy(bf16[2,1280,3072]{2,1,0:T(8,128)(2,1)S(1)} %pad_add_fusion.1) | data formatting | bytes 31457280
  404.9 15.5 %copy.29 = bf16[160,8,2,3072]{3,1,2,0:T(8,128)(2,1)} copy(bf16[160,8,2,3072]{3,2,1,0:T(2,128)(2,1)} %bitcast.93) | data formatting | bytes 31457280
  420.4 22.2 %fusion.31 = bf16[1,1280,3072]{2,1,0:T(8,128)(2,1)} fusion(bf16[2048,3072]{1,0:T(8,128)(2,1)} %get-tuple-element.28, bf16[2048,1280]{0,1:T(8,128)(2,1)} %copy-done.1, f32[2048]{0:T(1024)S(1)} %fusion.109), kind=kOutput, calls=%fused_computation.51 | convolution fusion | flops 16113991680 | bytes 25698304 | tf_op jit(solution)/shard_map/transpose(jvp())/dot_general | solution.py:26
  442.6 32.0 %fusion.28 = bf16[1,1280,3072]{2,1,0:T(8,128)(2,1)} fusion(f32[2048,3072]{1,0:T(8,128)} %fusion.49, f32[2048,3072]{1,0:T(8,128)} %get-tuple-element.25, bf16[2048,3072]{1,0:T(8,128)(2,1)} %convolution_convert_fusion.1, bf16[1,2048,1280]{1,2,0:T(8,128)(2,1)} %copy.22, f32[2048]{0:T(1024)S(1)} %copy-done.8), kind=kOutput, calls=%fused_computation.50 | convolution fusion | flops 16187129856 | bytes 76029952 | tf_op jit(solution)/shard_map/transpose(jvp())/dot_general | solution.py:26
  474.6 7.5 pad_add_fusion.2
  482.1 72.1 %copy.24 = bf16[2,1280,3072]{2,0,1:T(2,128)(2,1)} copy(bf16[2,1280,3072]{2,1,0:T(8,128)(2,1)S(1)} %pad_add_fusion.2) | data formatting | bytes 31457280
  554.1 15.5 %copy.28 = bf16[160,8,2,3072]{3,1,2,0:T(8,128)(2,1)} copy(bf16[160,8,2,3072]{3,2,1,0:T(2,128)(2,1)} %bitcast.94) | data formatting | bytes 31457280
  569.7 22.3 %fusion.35 = bf16[1,3072,1280]{2,1,0:T(8,128)(2,1)} fusion(bf16[2048,3072]{1,0:T(8,128)(2,1)} %get-tuple-element.24, bf16[2048,1280]{0,1:T(8,128)(2,1)} %fusion.76), kind=kOutput, calls=%fused_computation.55 | convolution fusion | flops 16110059520 | bytes 25690112 | tf_op jit(solution)/shard_map/transpose(jvp())/dot_general | solution.py:15
  592.0 28.6 %fusion.34 = bf16[1,3072,1280]{2,1,0:T(8,128)(2,1)} fusion(f32[2048,3072]{1,0:T(8,128)} %fusion.41, bf16[1,2048,1280]{2,1,0:T(8,128)(2,1)} %param.12, f32[2048,3072]{1,0:T(8,128)} %get-tuple-element.29), kind=kOutput, calls=%fused_computation.54 | convolution fusion | flops 16147808256 | bytes 63438848 | tf_op jit(solution)/shard_map/transpose(jvp())/dot_general | solution.py:15
  620.6 13.0 %pad_add_fusion = bf16[2,3072,1280]{2,1,0:T(8,128)(2,1)} fusion(bf16[1,3072,1280]{2,1,0:T(8,128)(2,1)} %fusion.35, bf16[1,3072,1280]{2,1,0:T(8,128)(2,1)} %fusion.34), kind=kLoop, calls=%fused_computation.26 | loop fusion | flops 7864320 | bytes 31457280 | tf_op jit(solution)/shard_map/transpose(jvp())/add_any | solution.py:45
  635.2 135.1 %reduce-scatter.10.cloned.1.call-done = bf16[40,6144]{1,0:T(8,128)(2,1)} async-done(((bf16[1280,6144]{1,0:T(8,128)(2,1)}), bf16[40,6144]{1,0:T(8,128)(2,1)}) %reduce-scatter.10.cloned.1.call-update) | async-done | bytes 491536
  774.6 172.3 %reduce-scatter.8.cloned.1.call-done = bf16[2,96,1280]{2,1,0:T(8,128)(2,1)} async-done(((bf16[2,3072,1280]{2,1,0:T(8,128)(2,1)}), bf16[2,96,1280]{2,1,0:T(8,128)(2,1)}) %reduce-scatter.8.cloned.1.call-update) | async-done | bytes 491536 | tf_op jit(solution)/shard_map/reduce_scatter | solution.py:135
  949.5 40.9 %psum.7 = f32[]{:T(128)} all-reduce(f32[]{:T(128)S(6)} %add.110), channel_id=1, replica_groups=mesh['rep'=1,'dp'=32] {'dp'}, use_global_device_ids=true, to_apply=%region_9.10 | all-reduce | flops 1 | bytes 8 | tf_op jit(solution)/shard_map/psum | solution.py:136
  999.2 194.1 %shard_map.178 = (bf16[2,2,2,2,2,2,40,3072]{7,6,5,4,3,2,1,0:T(8,128)(2,1)}, bf16[2,2,2,2,2,2,40,3072]{7,6,5,4,3,2,1,0:T(8,128)(2,1)}, bf16[2,2,2,2,2,2,96,1280]{7,6,5,4,3,2,1,0:T(8,128)(2,1)}) custom-call(bf16[2,40,3072]{2,1,0:T(8,128)(2,1)} %get-tuple-element.21.refs_0_, bf16[2,40,3072]{2,1,0:T(8,128)(2,1)} %get-tuple-element.32.refs_1_, ...), custom_call_target="tpu_custom_call" | custom-call | tf_op jit(solution)/shard_map/pallas_call | solution.py:121
  1193.4 15.9 %copy.43 = bf16[2,1280,3072]{2,1,0:T(8,128)(2,1)} copy(bf16[2,1280,3072]{2,1,0:T(8,128)(2,1)} %bitcast.101) | data formatting | bytes 31457280
  1209.3 8.0 copy.44
  1219.6 5.8 copy.45
  (55 shorter events, 23.3 us)
Async XLA Ops:
  7.2 626.5 %reduce-scatter.12.cloned.1.call-start = ((), (), s32[]{:S(2)}) async-start(), calls=%async_computation.5 | async-start | bytes 16220160
  18.7 52.1 %copy-start.7 = (f32[2048]{0:T(1024)}, f32[2048]{0:T(1024)S(1)}, u32[]{:S(2)}) copy-start(f32[2048]{0:T(1024)S(1)} %add_rsqrt_fusion) | copy-start | bytes 24580
  18.7 30.4 %slice-start.6 = ((s8[5242880]{0:T(1024)(128)(4,1)}), s8[1048576]{0:T(1024)(128)(4,1)S(1)}, s32[]{:S(2)}) async-start(s8[5242880]{0:T(1024)(128)(4,1)} %bitcast.102), calls=%async_computation.12 | async-start | bytes 2097152
  26.7 22.4 %slice-start.7 = ((s8[5242880]{0:T(1024)(128)(4,1)}), s8[4194304]{0:T(1024)(128)(4,1)S(1)}, s32[]{:S(2)}) async-start(s8[5242880]{0:T(1024)(128)(4,1)} %bitcast.102), calls=%async_computation.13 | async-start | bytes 8388608
  128.3 0.6 copy-start.5
  128.3 2.3 copy-start.1
  191.2 22.7 %copy-start.2 = (bf16[2048,1280]{0,1:T(8,128)(2,1)S(1)}, bf16[2048,1280]{0,1:T(8,128)(2,1)}, u32[]{:S(2)}) copy-start(bf16[2048,1280]{0,1:T(8,128)(2,1)} %copy-done.1) | copy-start | bytes 15728644
  237.6 28.5 %copy-start.6 = (f32[2048]{0:T(1024)S(1)}, f32[2048]{0:T(1024)}, u32[]{:S(2)}) copy-start(f32[2048]{0:T(1024)} %copy-done.5) | copy-start | bytes 24580
  266.1 35.5 %slice-start = ((s8[5242880]{0:T(1024)(128)(4,1)}), s8[1048576]{0:T(1024)(128)(4,1)S(1)}, s32[]{:S(2)}) async-start(s8[5242880]{0:T(1024)(128)(4,1)} %bitcast.95), calls=%async_computation.6 | async-start | bytes 2097152
  278.6 23.0 %slice-start.1 = ((s8[5242880]{0:T(1024)(128)(4,1)}), s8[4194304]{0:T(1024)(128)(4,1)S(1)}, s32[]{:S(2)}) async-start(s8[5242880]{0:T(1024)(128)(4,1)} %bitcast.95), calls=%async_computation.7 | async-start | bytes 8388608
  278.6 23.0 %copy-start.8 = (f32[2048]{0:T(1024)S(1)}, f32[2048]{0:T(1024)}, u32[]{:S(2)}) copy-start(f32[2048]{0:T(1024)} %copy-done.7) | copy-start | bytes 24580
  420.4 349.9 %reduce-scatter.10.cloned.1.call-start = ((), (), s32[]{:S(2)}) async-start(), calls=%async_computation.4 | async-start | bytes 16220160
  569.6 377.3 %reduce-scatter.8.cloned.1.call-start = ((), (), s32[]{:S(2)}) async-start(), calls=%async_computation.3 | async-start | bytes 16220160 | tf_op jit(solution)/shard_map/reduce_scatter | solution.py:135
  633.6 362.8 %copy-start.3 = (f32[2,96,1280]{2,1,0:T(8,128)S(1)}, f32[2,96,1280]{2,1,0:T(8,128)}, u32[]{:S(2)}) copy-start(f32[2,96,1280]{2,1,0:T(8,128)} %param.21) | copy-start | bytes 2949124
  633.6 362.8 %copy-start.4 = (f32[2,96,1280]{2,1,0:T(8,128)S(1)}, f32[2,96,1280]{2,1,0:T(8,128)}, u32[]{:S(2)}) copy-start(f32[2,96,1280]{2,1,0:T(8,128)} %param.18) | copy-start | bytes 2949124
  1193.4 15.9 %copy-start = (bf16[2,2,2,2,2,2,40,3072]{7,6,5,4,3,2,1,0:T(8,128)(2,1)S(1)}, bf16[2,2,2,2,2,2,40,3072]{7,6,5,4,3,2,1,0:T(8,128)(2,1)}, u32[]{:S(2)}) copy-start(bf16[2,2,2,2,2,2,40,3072]{7,6,5,4,3,2,1,0:T(8,128)(2,1)} %get-tuple-element.13) | copy-start | bytes 47185924
  1193.4 23.9 %slice-start.2 = ((s8[15728640]{0:T(1024)(128)(4,1)}), s8[4194304]{0:T(1024)(128)(4,1)S(1)}, s32[]{:S(2)}) async-start(s8[15728640]{0:T(1024)(128)(4,1)} %bitcast.97), calls=%async_computation.8 | async-start | bytes 8388608
  1193.4 23.9 %slice-start.3 = ((s8[15728640]{0:T(1024)(128)(4,1)}), s8[4194304]{0:T(1024)(128)(4,1)S(1)}, s32[]{:S(2)}) async-start(s8[15728640]{0:T(1024)(128)(4,1)} %bitcast.97), calls=%async_computation.9 | async-start | bytes 8388608
  1209.3 9.5 slice-start.4
  1209.3 10.4 slice-start.5
Sparse Core Ops, SparseCore 0:
  420.5 172.9 reduce-scatter.11
  600.1 170.1 reduce-scatter.9
  776.8 170.0 reduce-scatter.7

commit v2 on v1

v2 whole, which is shorter than its diff:
```python
import functools

import jax
import jax.numpy as jnp
from jax import lax
from jax.experimental import pallas as pl
from jax.experimental.pallas import tpu as pltpu
from jax.sharding import PartitionSpec as P

FB = 256
MB = 1024
VMEM_LIMIT = 67_000_000
def nt(a, b): return lax.dot_general(a, b, (((1,), (1,)), ((), ())), preferred_element_type=jnp.float32)
def nn(a, b): return lax.dot_general(a, b, (((1,), (0,)), ((), ())), preferred_element_type=jnp.float32)
def one(shape): return pl.BlockSpec(shape, lambda *_: (0,) * len(shape), pipeline_mode=pl.Buffered(1))
def normed(h):
    wide = h.astype(jnp.float32)
    return (wide * lax.rsqrt(jnp.mean(wide**2, -1, keepdims=True) + 1e-6)).astype(jnp.bfloat16)
def silu_parts(g):
    s = 0.5 * jnp.tanh(0.5 * g) + 0.5
    return s, g * s

ROWS = 512
def f0_kernel(n, x, wg, wu, wd, g, u, actT, aT0, h1, a1, aT1, a, acc):
    j = pl.program_id(0)
    rows = x.shape[0]
    def block(r): return pl.ds(pl.multiple_of(r * ROWS, ROWS), ROWS)
    @pl.when(j == 0)
    def _():
        acc[...] = jnp.zeros_like(acc)
        @pl.loop(0, rows // ROWS)
        def _(r): a[block(r), :] = normed(x[block(r), :])
    @pl.when((j > 0) & (j <= rows // ROWS))
    def _(): aT0[...] = a[block(j - 1), :].T
    @pl.when(j < n)
    def _():
        for m in range(0, rows, MB):
            s = slice(m, m + MB)
            gg = nn(a[s, :], wg[0]); g[0, s, :] = gg
            uu = nn(a[s, :], wu[0]); u[0, s, :] = uu
            act = (silu_parts(gg)[1] * uu).astype(jnp.bfloat16)
            actT[:, s] = act.T
            acc[s, :] += nn(act, wd[0])
    @pl.when(j >= n)
    def _():
        s = block(j - n)
        h = x[s, :] + acc[s, :].astype(jnp.bfloat16)
        h1[...] = h
        b = normed(h)
        a1[...] = b
        aT1[...] = b.T
def f0_call(x, wg, wu, wd, layer=0):
    t, d = x.shape; ff = wg.shape[2]; n = ff // FB; k = t // ROWS
    bf, f32 = jnp.bfloat16, jnp.float32
    cur = lambda j: jnp.minimum(j, n - 1)
    end = lambda j: jnp.maximum(j - n, 0)
    return pl.pallas_call(functools.partial(f0_kernel, n), grid=(n + k,),
        in_specs=[one((t, d)), pl.BlockSpec((1, d, FB), lambda j: (layer, 0, cur(j))), pl.BlockSpec((1, d, FB), lambda j: (layer, 0, cur(j))),
                  pl.BlockSpec((1, FB, d), lambda j: (layer, cur(j), 0))],
        out_specs=[pl.BlockSpec((1, t, FB), lambda j: (cur(j), 0, 0)), pl.BlockSpec((1, t, FB), lambda j: (cur(j), 0, 0)), pl.BlockSpec((FB, t), lambda j: (cur(j), 0)),
                   pl.BlockSpec((d, ROWS), lambda j: (0, jnp.clip(j - 1, 0, k - 1))),
                   pl.BlockSpec((ROWS, d), lambda j: (end(j), 0)), pl.BlockSpec((ROWS, d), lambda j: (end(j), 0)), pl.BlockSpec((d, ROWS), lambda j: (0, end(j)))],
        out_shape=[jax.ShapeDtypeStruct((n, t, FB), f32)] * 2 + [jax.ShapeDtypeStruct((ff, t), bf), jax.ShapeDtypeStruct((d, t), bf),
                   jax.ShapeDtypeStruct((t, d), bf), jax.ShapeDtypeStruct((t, d), bf), jax.ShapeDtypeStruct((d, t), bf)],
        scratch_shapes=[pltpu.VMEM((t, d), bf), pltpu.VMEM((t, d), f32)],
        compiler_params=pltpu.CompilerParams(vmem_limit_bytes=VMEM_LIMIT))(x, wg, wu, wd)
def f1_kernel(a, dy, wg, wu, g, u, dwd, actT):
    for m in range(0, a.shape[0], MB):
        s = slice(m, m + MB)
        gg = nn(a[s, :], wg[0]); g[0, s, :] = gg
        uu = nn(a[s, :], wu[0]); u[0, s, :] = uu
        actT[:, s] = (silu_parts(gg)[1] * uu).astype(jnp.bfloat16).T
    dwd[...] = nn(actT[...], dy[...]).astype(jnp.bfloat16)
def f1_call(a, dy, wg, wu, layer=1):
    t, d = a.shape; ff = wg.shape[2]; n = ff // FB
    bf, f32 = jnp.bfloat16, jnp.float32
    return pl.pallas_call(f1_kernel, grid=(n,),
        in_specs=[one((t, d)), one((t, d)), pl.BlockSpec((1, d, FB), lambda j: (layer, 0, j)), pl.BlockSpec((1, d, FB), lambda j: (layer, 0, j))],
        out_specs=[pl.BlockSpec((1, t, FB), lambda j: (j, 0, 0)), pl.BlockSpec((1, t, FB), lambda j: (j, 0, 0)), pl.BlockSpec((FB, d), lambda j: (j, 0))],
        out_shape=[jax.ShapeDtypeStruct((n, t, FB), f32)] * 2 + [jax.ShapeDtypeStruct((ff, d), bf)],
        scratch_shapes=[pltpu.VMEM((FB, t), bf)],
        compiler_params=pltpu.CompilerParams(vmem_limit_bytes=VMEM_LIMIT))(a, dy, wg, wu)


MESHID = pl.DeviceIdType.MESH
def place():
    me = lax.axis_index("dp")
    return (me // 16) % 2, (me // 8) % 2, (me // 4) % 2, (me // 2) % 2, me % 2
MASK = (16, 8, 4, 2, 1)
def partner(pos, dim):
    me = lax.axis_index("dp")
    return me + MASK[dim] * (1 - 2 * pos[dim])
def dev(i): return {"rep": 0, "dp": i}
X, Y, ZH, ZL, C = range(5)
LAG = 2
GATHER = ((ZH, ZL, Y, X, C), (ZH, X, ZL, Y, C), (ZH, Y, X, ZL, C))

def barrier(pos, dims):
    bar = pltpu.get_barrier_semaphore()
    for d in dims:
        pl.semaphore_signal(bar, inc=1, device_id=dev(partner(pos, d)), device_id_type=MESHID)
    pl.semaphore_wait(bar, len(dims))

def streams(sizes):
    groups = []
    for layer in (0, 1):
        for i in (0, 1, 2):
            for lo, parts in sizes[i]:
                g = []
                for colour, n in enumerate(parts):
                    g.append((i, layer, lo, n, colour)); lo += n
                groups.append(g)
    return groups

def gather_kernel(groups, own, out, send, recv, local):
    pos = place()
    barrier(pos, range(5))
    me = tuple(pos)
    first = []
    for i in range(3):
        cp = pltpu.make_async_copy(own[i], out[i].at[(slice(None), *me)], local.at[i]); cp.start(); first.append(cp)
    def copy(n, s, phase):
        i, layer, lo, cols, colour = s
        order = GATHER[colour]
        done = order[:phase]
        d = order[phase]
        cs = pl.ds(lo, cols)
        if phase == 0:
            src = own[i].at[layer, :, cs]
        index = (layer, *(slice(None) if k in done else pos[k] for k in range(5)), slice(None), cs)
        dst = out[i].at[index]
        if phase: src = dst
        return pltpu.make_async_remote_copy(src_ref=src, dst_ref=dst, send_sem=send.at[n, phase], recv_sem=recv.at[n, phase],
                                            device_id=dev(partner(pos, d)), device_id_type=MESHID)
    started = []
    for k in range(len(groups) + 5 * LAG):
        for g in range(len(groups)):
            phase, odd = divmod(k - g, LAG)
            if 0 <= phase <= 5 and not odd:
                for j, s in enumerate(groups[g]):
                    n = 3 * g + j
                    if phase > 0: copy(n, s, phase - 1).wait_recv()
                    if phase == 1 and g == 0 and j == 0:
                        for cp in first: cp.wait()
                    if phase < 5:
                        c = copy(n, s, phase); c.start(); started.append(c)
    for c in started: c.wait_send()

WIDE = tuple((lo, (384, 384, 256)) for lo in (0, 1024, 2048))
NARROW = tuple((lo, (256, 256, 128)) for lo in (0, 640))
SIZES = (WIDE, WIDE, NARROW)
def gather(own, sizes=SIZES):
    groups = streams(sizes)
    n = 3 * len(groups)
    def kernel(*refs):
        gather_kernel(groups, refs[:3], refs[3:6], *refs[6:])
    out = pl.pallas_call(kernel,
        out_shape=[jax.ShapeDtypeStruct((2, 2, 2, 2, 2, 2, *o.shape[1:]), o.dtype) for o in own],
        in_specs=[pl.BlockSpec(memory_space=pltpu.VMEM)] * 3, out_specs=[pl.BlockSpec(memory_space=pl.ANY)] * 3,
        scratch_shapes=[pltpu.SemaphoreType.DMA((n, 5)), pltpu.SemaphoreType.DMA((n, 5)), pltpu.SemaphoreType.DMA((3,))],
        compiler_params=pltpu.CompilerParams(vmem_limit_bytes=20_000_000, collective_id=3, has_side_effects=True))(*own)
    return [o.reshape(2, -1, o.shape[-1]) for o in out]


ORDER = ((X, Y, ZL), (Y, ZL, X), (ZL, X, Y))
AFTER = (1, 3, 5, 7, 9)
DRAIN = AFTER[-1]

def two(q): return lax.rem(q, 2)
def four(q): return lax.rem(q, 4)
def dmas(*n): return pltpu.SemaphoreType.DMA(n)

class Stream:
    def __init__(self, half, lanes, cuts, count, first):
        self.half, self.lanes, self.cuts, self.count, self.first = half, lanes, cuts, count, first
    def scratch(self):
        r, n, bf = 2 * self.half, self.lanes, jnp.bfloat16
        rows = [b - a for a, b in zip(self.cuts, self.cuts[1:])]
        shapes = [pltpu.VMEM((2, 8, r, n), bf), pltpu.VMEM((2, 8, r, n), bf)]
        for rc in rows:
            for k in (8, 4, 2): shapes += [pltpu.VMEM((4, k, rc, n), bf), pltpu.VMEM((4, k // 2, rc, n), bf)]
        shapes += [pltpu.VMEM((4, r, n), jnp.float32), pltpu.VMEM((4, self.half, n), bf), pltpu.VMEM((4, self.half, n), bf)]
        shapes += [dmas(2), dmas(2), dmas(3, 3, 4), dmas(3, 3, 4),
                   dmas(4), dmas(4)]
        return shapes
    def bind(self, refs, pos, squares, store):
        self.pos, self.squares, self.store = pos, squares, store
        self.made, self.got = refs[0], refs[1]
        self.colours = [refs[2 + 6 * k : 8 + 6 * k] for k in range(3)]
        self.last, self.zsend, self.zgot, self.cs, self.cr, self.ps, self.pr, self.zs, self.zr = refs[20:]
        return self
    def core_copy(self, q):
        slot = two(q)
        return pltpu.make_async_remote_copy(src_ref=self.made.at[1 - self.pos[C]], dst_ref=self.got.at[slot], send_sem=self.cs.at[slot], recv_sem=self.cr.at[slot],
                                            device_id=dev(partner(self.pos, C)), device_id_type=MESHID)
    def chip_copy(self, colour, phase, q):
        slot = four(q)
        n = 8 >> phase
        d = ORDER[colour][phase]
        src = self.colours[colour][2 * phase].at[slot, pl.ds((1 - self.pos[d]) * (n // 2), n // 2)]
        dst = self.colours[colour][2 * phase + 1].at[slot]
        return pltpu.make_async_remote_copy(src_ref=src, dst_ref=dst, send_sem=self.ps.at[phase, colour, slot], recv_sem=self.pr.at[phase, colour, slot],
                                            device_id=dev(partner(self.pos, d)), device_id_type=MESHID)
    def z_copy(self, q):
        slot = four(q)
        return pltpu.make_async_remote_copy(src_ref=self.zsend.at[slot], dst_ref=self.zgot.at[slot], send_sem=self.zs.at[slot], recv_sem=self.zr.at[slot],
                                            device_id=dev(partner(self.pos, ZH)), device_id_type=MESHID)
    def send(self, t):
        q = t - self.first
        @pl.when((q >= 0) & (q < self.count))
        def _(): self.core_copy(q).start()
    def when(self, t, p, body):
        q = t - self.first - AFTER[p]
        @pl.when((q >= 0) & (q < self.count))
        def _(): body(q)
    def advance(self, t, stage):
        pos, f32, bf = self.pos, jnp.float32, jnp.bfloat16
        def finish(q):
            slot = four(q)
            self.z_copy(q).wait()
            keep = self.last[slot, pl.ds(pl.multiple_of(pos[ZH] * self.half, 8), self.half), :]
            total = (keep + self.zgot[slot].astype(f32)).astype(bf)
            self.store(q, total)
            square = total.astype(f32) ** 2
            square = sum(square[:, k : k + 128] for k in range(0, self.lanes, 128))
            self.squares[...] += sum(square[k : k + 8] for k in range(0, self.half, 8))
        def third(q):
            slot = from_ = four(q)
            for k in range(3):
                self.chip_copy(k, 2, q).wait()
                a, b = self.cuts[k], self.cuts[k + 1]
                s, r = self.colours[k][4:6]
                self.last[slot, a:b, :] = s[from_, pos[ORDER[k][2]]].astype(f32) + r[from_, 0].astype(f32)
            self.zsend[slot] = self.last[slot, pl.ds(pl.multiple_of((1 - pos[ZH]) * self.half, 8), self.half), :].astype(bf)
            self.z_copy(q).start()
        def second(q):
            slot = four(q)
            for k in range(3):
                self.chip_copy(k, 1, q).wait()
                s, r, s2 = self.colours[k][2:5]
                for i in range(2):
                    s2[slot, i] = (s[slot, 2 * pos[ORDER[k][1]] + i].astype(f32) + r[slot, i].astype(f32)).astype(bf)
                self.chip_copy(k, 2, q).start()
        def first(q):
            slot = into = four(q)
            for k in range(3):
                self.chip_copy(k, 0, q).wait()
                s, r, s2 = self.colours[k][:3]
                for i in range(4):
                    s2[into, i] = (s[slot, 4 * pos[ORDER[k][0]] + i].astype(f32) + r[slot, i].astype(f32)).astype(bf)
                self.chip_copy(k, 1, q).start()
        def cores(q):
            slot, into = two(q), four(q)
            self.core_copy(q).wait()
            @pl.loop(0, 8, unroll=4)
            def _(b):
                bits = {X: b // 4, Y: (b // 2) % 2, ZL: b % 2}
                total = (self.made[pos[C], b].astype(f32) + self.got[slot, b].astype(f32)).astype(bf)
                for k in range(3):
                    d = ORDER[k]
                    self.colours[k][0][into, 4 * bits[d[0]] + 2 * bits[d[1]] + bits[d[2]]] = total[self.cuts[k] : self.cuts[k + 1]]
            for k in range(3): self.chip_copy(k, 0, q).start()
        self.when(t, stage, (cores, first, second, third, finish)[stage])
    def put(self, whole, x=None):
        h = self.half
        for c in range(2):
            for b in range(8 if x is None else 4):
                r = ((b // 2) * 8 + (b % 2) * 2 + c) * h
                parts = [whole[r + zh * 4 * h : r + (zh * 4 + 1) * h, :] for zh in range(2)]
                self.made[c, b + 4 * (x or 0)] = jnp.concatenate(parts, 0).astype(jnp.bfloat16)

def advance(t, *streams):
    for stage in (4, 3, 2, 1, 0):
        for one_of in streams: one_of.advance(t, stage)

def elem(dact, g, u):
    dact = dact.astype(jnp.bfloat16).astype(jnp.float32)
    s, silu = silu_parts(g)
    return (dact * u * (s * (1 + g - silu))).astype(jnp.bfloat16), (dact * silu).astype(jnp.bfloat16)

NROWS = 256
TILE = (8, 128)
def before_gates(dy, wd, g, u, dgu):
    for m in range(0, dy.shape[0], EB):
        s = slice(m, m + EB)
        dgu[s, :FB], dgu[s, FB:] = elem(nt(dy[s, :], wd[0]), g[0, s, :], u[0, s, :])

EB, AB = 256, 512
CUT40, CUT96 = (0, 32, 64, 80), (0, 80, 144, 192)

def store_in(out, width):
    def store(q, total): out[:, pl.ds(pl.multiple_of(q * width, width), width)] = total
    return store
def store_pair(gate, up):
    def store(q, total):
        s = pl.ds(pl.multiple_of(q * FB, FB), FB)
        gate[:, s] = total[:, :FB]
        up[:, s] = total[:, FB:]
    return store
def b1_kernel(n, aT, dy, h1, g, u, wg, wu, wd, dwd, dh, out_g, out_u, out_d, squares, dgu, acc, tmp, *refs):
    t = pl.program_id(0)
    pos = place()
    G = Stream(40, 2 * FB, CUT40, n, 0); Dn = Stream(96, 128, CUT96, n - 2, 0)
    ng = len(G.scratch())
    G.bind(refs[:ng], pos, squares, store_pair(out_g, out_u)); Dn.bind(refs[ng:], pos, squares, store_in(out_d, 128))
    @pl.when(t == 0)
    def _():
        barrier(pos, range(5))
        acc[...] = jnp.zeros_like(acc)
        squares[...] = jnp.zeros_like(squares)
    @pl.when(t < n)
    def _():
        before_gates(dy, wd, g, u, dgu)
    advance(t, Dn, G)
    @pl.when(t < Dn.count)
    def _(): Dn.put(dwd)
    Dn.send(t)
    @pl.when(t < n)
    def _():
        tmp[...] = nn(aT[...], dgu[...])
        G.put(tmp)
        for m in range(0, dy.shape[0], AB):
            s = slice(m, m + AB)
            acc[s, :] += nt(dgu[s, :FB], wg[0]) + nt(dgu[s, FB:], wu[0])
    G.send(t)
    @pl.when((t >= n) & (t < n + dy.shape[0] // NROWS))
    def _():
        s = pl.ds(pl.multiple_of((t - n) * NROWS, NROWS), NROWS)
        wide, da = h1[...].astype(jnp.float32), acc[s, :].astype(jnp.bfloat16).astype(jnp.float32)
        scale = lax.rsqrt(jnp.mean(wide**2, -1, keepdims=True) + 1e-6)
        dwide = da * scale - wide * (scale * scale * scale * jnp.mean(da * wide, -1, keepdims=True))
        dh[...] = dy[s, :] + dwide.astype(jnp.bfloat16)

def b1_call(aT, dy, h1, g, u, wg, wu, wd, dwd, layer=1):
    d, tk = aT.shape; ff = wg.shape[2]; n = ff // FB; k = tk // NROWS
    G = Stream(40, 2 * FB, CUT40, n, 0); Dn = Stream(96, 128, CUT96, n - 2, 0)
    bf, f32 = jnp.bfloat16, jnp.float32
    own = [(G.half, ff), (G.half, ff), (Dn.half, d)]
    cur = lambda j: jnp.minimum(j, n - 1)
    end = lambda j: jnp.clip(j - n, 0, k - 1)
    return pl.pallas_call(functools.partial(b1_kernel, n), grid=(n + DRAIN,),
        in_specs=[one((d, tk)), one((tk, d)), pl.BlockSpec((NROWS, d), lambda j: (end(j), 0)),
                  pl.BlockSpec((1, tk, FB), lambda j: (cur(j), 0, 0)), pl.BlockSpec((1, tk, FB), lambda j: (cur(j), 0, 0)),
                  pl.BlockSpec((1, d, FB), lambda j: (layer, 0, cur(j))), pl.BlockSpec((1, d, FB), lambda j: (layer, 0, cur(j))), pl.BlockSpec((1, FB, d), lambda j: (layer, cur(j), 0)),
                  pl.BlockSpec((ff, 128), lambda j: (0, jnp.minimum(j, n - 3)))],
        out_specs=[pl.BlockSpec((NROWS, d), lambda j: (end(j), 0)), *map(one, own), one(TILE)],
        out_shape=[jax.ShapeDtypeStruct((tk, d), bf), *[jax.ShapeDtypeStruct(o, bf) for o in own], jax.ShapeDtypeStruct(TILE, f32)],
        scratch_shapes=[pltpu.VMEM((tk, 2 * FB), bf), pltpu.VMEM((tk, d), f32), pltpu.VMEM((d, 2 * FB), f32)] + G.scratch() + Dn.scratch(),
        compiler_params=pltpu.CompilerParams(vmem_limit_bytes=VMEM_LIMIT, collective_id=1, has_side_effects=True))(aT, dy, h1, g, u, wg, wu, wd, dwd)

def others(dims):
    me, pos = lax.axis_index("dp"), place()
    for which in range(1, 1 << len(dims)):
        yield me + sum(MASK[d] * (1 - 2 * pos[d]) for k, d in enumerate(dims) if which >> k & 1)
def greet(groups):
    bar = pltpu.get_barrier_semaphore()
    count = 0
    for dims in groups:
        for other in others(dims):
            pl.semaphore_signal(bar, inc=1, device_id=dev(other), device_id_type=MESHID)
            count += 1
    pl.semaphore_wait(bar, count)
def everyone(value, got, send, recv, dims, first):
    pos = place()
    n = 1 << len(dims)
    mine = sum(pos[d] << k for k, d in enumerate(dims))
    copies = []
    for k, other in enumerate(others(dims)):
        copies.append(pltpu.make_async_remote_copy(src_ref=value, dst_ref=got.at[first + mine], send_sem=send.at[first + k], recv_sem=recv.at[first + k],
                                                   device_id=dev(other), device_id_type=MESHID))
    for c in copies: c.start()
    got[first + mine] = value[...]
    for c in copies: c.wait()
    value[...] = sum(got[first + k] for k in range(n))

def b0_kernel(n, nb, count, aT, dh, wd, squares1, g_all, u_all, actT, out_g, out_u, out_d, factor, g, u, gsem, tmp, dgu, act, asem, squares, sgot, ssend, srecv, *refs):
    t = pl.program_id(0)
    pos = place()
    G = Stream(40, 2 * FB, CUT40, n, 0); Dn = Stream(96, FB, CUT96, nb, 0)
    ng = len(G.scratch())
    G.bind(refs[:ng], pos, squares, store_pair(out_g, out_u)); Dn.bind(refs[ng:], pos, squares, store_in(out_d, FB))
    rows = act.shape[1]
    def fetch(b): return pltpu.make_async_copy(actT.at[b * rows : (b + 1) * rows, :], act.at[b], asem.at[b])
    def saved(j): return [pltpu.make_async_copy(a.at[j], b.at[0], gsem.at[k]) for k, (a, b) in enumerate(((g_all, g), (u_all, u)))]
    @pl.when(t == 0)
    def _():
        for b in range(4): fetch(b).start()
        for c in saved(0): c.start()
        greet(((X, Y, C), (ZH, ZL)))
        squares[...] = squares1[...]
    advance(t, Dn)
    @pl.when(t < nb)
    def _():
        columns = pl.ds(pl.multiple_of(t * FB, FB), FB)
        for xy in range(4):
            @pl.when(t == 0)
            def _(): fetch(xy).wait()
            for zh in range(2):
                value = nn(act[xy, zh * rows // 2 : (zh + 1) * rows // 2, :], dh[:, columns])
                for zl in range(2):
                    for c in range(2):
                        r = (zl * 2 + c) * 96
                        Dn.made[c, xy * 2 + zl, zh * 96 : zh * 96 + 96, :] = value[r : r + 96].astype(jnp.bfloat16)
    Dn.send(t)
    @pl.when(t < n)
    def _():
        for c in saved(t): c.wait()
        before_gates(dh, wd, g, u, dgu)
    @pl.when(t < n - 1)
    def _():
        for c in saved(t + 1): c.start()
    advance(t, G)
    @pl.when(t < n)
    def _():
        half = aT.shape[0] // 2
        for x in range(2):
            tmp[...] = nn(aT[x * half : (x + 1) * half, :], dgu[...])
            G.put(tmp, x)
    G.send(t)
    @pl.when(t == n + DRAIN - 1)
    def _():
        everyone(squares, sgot, ssend, srecv, (X, Y, C), 0)
        everyone(squares, sgot, ssend, srecv, (ZH, ZL), 8)
        total = jnp.sum(jnp.sum(squares[...], 1, keepdims=True), 0, keepdims=True)
        factor[...] = jnp.broadcast_to(jnp.minimum(1.0, 0.5 * lax.rsqrt(total / count + 1e-30)), factor.shape)

def b0_call(aT, dh, actT, g, u, wd, squares1, count, layer=0):
    d, tk = aT.shape; ff = wd.shape[1]; n = ff // FB; nb = d // FB
    G = Stream(40, 2 * FB, CUT40, n, 0); Dn = Stream(96, FB, CUT96, nb, 0)
    bf, f32 = jnp.bfloat16, jnp.float32
    own = [(G.half, ff), (G.half, ff), (Dn.half, d)]
    cur = lambda j: jnp.minimum(j, n - 1)
    return pl.pallas_call(functools.partial(b0_kernel, n, nb, count), grid=(n + DRAIN,),
        in_specs=[one((d, tk)), one((tk, d)),
                  pl.BlockSpec((1, FB, d), lambda j: (layer, cur(j), 0)), one(TILE), *[pl.BlockSpec(memory_space=pl.ANY)] * 3],
        out_specs=[*map(one, own), one(TILE)],
        out_shape=[*[jax.ShapeDtypeStruct(o, bf) for o in own], jax.ShapeDtypeStruct(TILE, f32)],
        scratch_shapes=[*[pltpu.VMEM((1, tk, FB), f32)] * 2, dmas(2), pltpu.VMEM((d // 2, 2 * FB), f32), pltpu.VMEM((tk, 2 * FB), bf), pltpu.VMEM((4, ff // 4, tk), bf), dmas(4),
                        pltpu.VMEM(TILE, f32), pltpu.VMEM((12, *TILE), f32), dmas(12), dmas(12)] + G.scratch() + Dn.scratch(),
        compiler_params=pltpu.CompilerParams(vmem_limit_bytes=VMEM_LIMIT, collective_id=2, has_side_effects=True))(aT, dh, wd, squares1, g, u, actT)


def adamw(w, m, v, g):
    m = 0.9 * m + 0.1 * g
    v = 0.95 * v + 0.05 * g * g
    step = m * lax.rsqrt(v + 1e-8) + 0.1 * w
    return (w - 0.02 * step).astype(jnp.bfloat16), m, v


def solution(mesh):
    def step(x, dy, *arrays):
        weights, m, v = (arrays[i : i + 3] for i in (0, 3, 6))
        x, dy = x[0], dy[0]
        wg, wu, wd = weights
        g0, u0, actT0, aT0, h1, a1, aT1 = f0_call(x, wg, wu, wd)
        g1, u1, dwd1 = f1_call(a1, dy, wg, wu)
        dh1, *of1, squares1 = b1_call(aT1, dy, h1, g1, u1, wg, wu, wd, dwd1)
        *of0, factor = b0_call(aT0, dh1, actT0, g0, u0, wd, squares1, sum(w.size for w in weights))
        gradients = [jnp.stack([a, b]).astype(jnp.float32) for a, b in zip(of0, of1)]
        factor = factor[0, 0]
        me = lax.axis_index("dp")
        own = [lax.dynamic_slice_in_dim(w, me * g.shape[1], g.shape[1], 1) for w, g in zip(weights, gradients)]
        new = [adamw(w.astype(jnp.float32), m, v, g * factor) for w, m, v, g in zip(own, m, v, gradients, strict=True)]
        full = gather([one[0] for one in new])
        return (*full, *(one[1] for one in new), *(one[2] for one in new))

    data, whole, shard = P(("rep", "dp")), P(), P(None, "dp")
    return jax.shard_map(
        step,
        mesh=mesh,
        in_specs=(data, data, *[whole] * 3, *[shard] * 6),
        out_specs=(*[P("rep")] * 3, *[P("rep", "dp")] * 6),
        check_vma=False,
    )
```

time: 1240 us -> 619 us (0.50)
  matrix products: 389 us -> 0 us
  Pallas kernels: 194 us -> 583 us
  waiting for transfers between devices: 307 us -> 0 us
  local copies, waits for them, and re-layouts: 228 us -> 24 us
  other arithmetic: 55.9 us -> 10.4 us
  blocking collectives: 40.9 us -> 0 us
  between operations: 17.1 us -> 0.69 us
    pallas_call x0 -> x4, Pallas kernels: none -> 400 us  [the longest x1 140 us: b1_call(): pl.pallas_call(functools.partial(b1_kernel, n), grid=(n + DRAIN,), in_spe...]
    dot_general x15 -> x0, matrix products: 389 us -> none  [the longest x5 137 us: layer(): gate = jnp.dot(a, w['w_gate'], preferred_element_type=jnp.float32)]
    unnamed x45 -> x11, local copies, waits for them, and re-layouts: 228 us -> 22.8 us
    reduce_scatter x1 -> x0, waiting for transfers between devices: 172 us -> none  [step(): lax.psum_scatter(by_weights[name], 'dp', scatter_dimension=1, tiled=True)]
    unnamed x5 -> x0, waiting for transfers between devices: 135 us -> none
    psum x1 -> x0, blocking collectives: 40.9 us -> none  [step(): squares = lax.psum(sum((jnp.sum(g * g) for g in gradients)), 'dp')]
    add_any x4 -> x0, other arithmetic: 40.5 us -> none  [the longest x3 28 us: stack(): h = layer(h, {name: w[number] for name, w in weights.items()})]
  transfers between devices with their start and end apart: 3 -> 0, of which waited for: 2 -> 0; matrix products, arithmetic and copies ran while one was open for 18% -> 0% of each run, Pallas kernels for 0% -> 0%
where the time goes in v2:
time: 619 us; the launch traced here: 618 us
  Pallas kernels  583 us (94%)
  local copies, waits for them, and re-layouts  24 us (4%)
  other arithmetic  10.4 us (2%)
    pallas_call x1, Pallas kernels, gather(): pl.pallas_call(kernel, out_shape=[jax.ShapeDtypeStruct((2, 2, 2, 2, 2, 2,...  183 us
    pallas_call x1, Pallas kernels, b1_call(): pl.pallas_call(functools.partial(b1_kernel, n), grid=(n + DRAIN,), in_spe...  140 us
    pallas_call x1, Pallas kernels, b0_call(): pl.pallas_call(functools.partial(b0_kernel, n, nb, count), grid=(n + DRAI...  131 us
    pallas_call x1, Pallas kernels, f0_call(): pl.pallas_call(functools.partial(f0_kernel, n), grid=(n + k,), in_specs=[...  70 us
    pallas_call x1, Pallas kernels, f1_call(): pl.pallas_call(f1_kernel, grid=(n,), in_specs=[one((t, d)), one((t, d)),...  59.1 us
    unnamed x11, local copies, waits for them, and re-layouts  22.8 us

profile of v2, /device:TPU:0, one launch (start us, length us, event | category | flops | bytes accessed | tf_op | source)
XLA Modules:
  0.0 618.4 jit_solution(12681701081514033632)
XLA Ops:
  0.6 70.0 %shard_map.178 = (f32[12,2048,256]{2,1,0:T(8,128)}, f32[12,2048,256]{2,1,0:T(8,128)}, bf16[3072,2048]{1,0:T(8,128)(2,1)}, bf16[1280,2048]{1,0:T(8,128)(2,1)}, bf...) custom-call(bf16[2048,1280]{1,0:T(8,128)(2,1)} %bitcast.19, ...), custom_call_target="tpu_custom_call" | custom-call | tf_op jit(solution)/shard_map/pallas_call | solution.py:57
  70.7 59.1 %shard_map.179 = (f32[12,2048,256]{2,1,0:T(8,128)}, f32[12,2048,256]{2,1,0:T(8,128)}, bf16[3072,1280]{1,0:T(8,128)(2,1)}) custom-call(bf16[2048,1280]{1,0:T(8,128)(2,1)} %get-tuple-element.34.a, bf16[2048,1280]{1,0:T(8,128)(2,1)} %bitcast.14, bf16[2,1280,3072]{2,1,0:T(8,128)(2,1)} %wg.5, bf16[2,1280,3072]{2,1,0:T(8,128)(2,1)} %wu.5), custom_call_target="tpu_custom_call" | custom-call | tf_op jit(solution)/shard_map/pallas_call | solution.py:77
  129.8 140.1 %shard_map.180 = (bf16[2048,1280]{1,0:T(8,128)(2,1)}, bf16[40,3072]{1,0:T(8,128)(2,1)}, bf16[40,3072]{1,0:T(8,128)(2,1)}, bf16[96,1280]{1,0:T(8,128)(2,1)}, f32[8,128]{1,0:T(8,128)}) custom-call(bf16[1280,2048]{1,0:T(8,128)(2,1)} %get-tuple-element.32.aT, bf16[2048,1280]{1,0:T(8,128)(2,1)} %bitcast.15, bf16[2048,1280]{1,0:T(8,128)(2,1)} %get-tuple-element.33.h1, ...), custom_call_target="tpu_custom_call" | custom-call | tf_op jit(solution)/shard_map/pallas_call | solution.py:341
  269.9 131.0 %shard_map.181 = (bf16[40,3072]{1,0:T(8,128)(2,1)}, bf16[40,3072]{1,0:T(8,128)(2,1)}, bf16[96,1280]{1,0:T(8,128)(2,1)}, f32[8,128]{1,0:T(8,128)}) custom-call(bf16[1280,2048]{1,0:T(8,128)(2,1)} %get-tuple-element.31.aT, bf16[2048,1280]{1,0:T(8,128)(2,1)} %get-tuple-element.38.dh, bf16[2,3072,1280]{2,1,0:T(8,128)(2,1)} %wd.5, ...), custom_call_target="tpu_custom_call" | custom-call | tf_op jit(solution)/shard_map/pallas_call | solution.py:433
  400.9 1.2 slice.3
  402.1 4.3 fusion.8
  406.5 6.1 fusion.2
  412.5 183.0 %shard_map.182 = (bf16[2,2,2,2,2,2,40,3072]{7,6,5,4,3,2,1,0:T(8,128)(2,1)S(1)}, bf16[2,2,2,2,2,2,40,3072]{7,6,5,4,3,2,1,0:T(8,128)(2,1)S(1)}, bf16[2,2,2,2,2,2,96,1280]{7,6,5,4,3,2,1,0:T(8,128)(2,1)}) custom-call(bf16[2,40,3072]{2,1,0:T(8,128)(2,1)S(1)} %get-tuple-element.59.refs_0_, bf16[2,40,3072]{2,1,0:T(8,128)(2,1)S(1)} %get-tuple-element.62.refs_1_, ...), custom_call_target="tpu_custom_call" | custom-call | tf_op jit(solution)/shard_map/pallas_call | solution.py:157
  595.6 0.0 slice-start
  595.6 0.0 slice-start.1
  595.6 7.8 %copy.23 = bf16[2,1280,3072]{2,1,0:T(8,128)(2,1)} copy(bf16[2,1280,3072]{2,1,0:T(8,128)(2,1)S(1)} %bitcast.13) | data formatting | bytes 31457280
  603.4 0.0 slice-start.2
  603.4 0.0 slice-start.3
  603.4 8.0 %copy.24 = bf16[2,1280,3072]{2,1,0:T(8,128)(2,1)} copy(bf16[2,1280,3072]{2,1,0:T(8,128)(2,1)S(1)} %bitcast.12) | data formatting | bytes 31457280
  611.3 0.0 slice-done
  611.3 0.0 slice-done.1
  611.3 0.0 slice-done.2
  611.3 1.2 slice-done.3
  612.6 5.8 copy.25
  (1 shorter events, 0.0 us)
Async XLA Ops:
  595.6 15.8 %slice-start = ((s8[15728640]{0:T(1024)(128)(4,1)}), s8[3145728]{0:T(1024)(128)(4,1)S(1)}, s32[]{:S(2)}) async-start(s8[15728640]{0:T(1024)(128)(4,1)} %bitcast.16), calls=%async_computation | async-start | bytes 6291456
  595.6 15.8 %slice-start.1 = ((s8[15728640]{0:T(1024)(128)(4,1)}), s8[4194304]{0:T(1024)(128)(4,1)S(1)}, s32[]{:S(2)}) async-start(s8[15728640]{0:T(1024)(128)(4,1)} %bitcast.16), calls=%async_computation.1 | async-start | bytes 8388608
  603.4 8.0 %slice-start.2 = ((s8[15728640]{0:T(1024)(128)(4,1)}), s8[4194304]{0:T(1024)(128)(4,1)S(1)}, s32[]{:S(2)}) async-start(s8[15728640]{0:T(1024)(128)(4,1)} %bitcast.16), calls=%async_computation.2 | async-start | bytes 8388608
  603.4 9.2 %slice-start.3 = ((s8[15728640]{0:T(1024)(128)(4,1)}), s8[4194304]{0:T(1024)(128)(4,1)S(1)}, s32[]{:S(2)}) async-start(s8[15728640]{0:T(1024)(128)(4,1)} %bitcast.16), calls=%async_computation.3 | async-start | bytes 8388608
